TPU v7x, 32 devices: a whole 2x2x4 slice. The times are simulated.
32 devices in a mesh: grid: 8 (over z, x), band: 4 (over y, core).
Axes of the slice: x: 2, y: 2, z: 4, core: 2. Of those that a mesh axis runs over, the one named last changes fastest.
Arguments:
- psi: bfloat16 [2048, 16, 512], P('band', 'grid'), may hold values from -6 to 6
- ritz_matrix: float32 [2048, 2048], P('band'), may hold values from -0.125 to 0.125
- potential: float32 [16, 512], P('grid'), may hold values from 0.5 to 10, as said below
Outputs:
- rotated: bfloat16 [2048, 16, 512], P('band', 'grid')
- search: bfloat16 [2048, 16, 512], P('band', 'grid')
Inputs may be any that keep to these rules, and one draw needn't show every extreme that they name: `potential`: positive everywhere.
All inputs are finite; a program needn't handle non-finite values.
Results may differ from a plain program's by a relative error of at most 0.0049.
Values may be sent and summed in bfloat16 or wider, within the bound.
A program may use at most 64 MiB of HBM per device.

v0:
```python
import jax
import jax.numpy as jnp
from jax import lax
from jax.sharding import PartitionSpec as P

NZ = 64
epsilon_mean = 1e-06


def with_halo(value, sides, width):
    for axis, dim in sides:
        count, length = (lax.axis_size(axis), value.shape[dim])
        up = [(i, (i + 1) % count) for i in range(count)]
        down = [(j, i) for i, j in up]
        last = lax.slice_in_dim(value, length - width, length, axis=dim)
        first = lax.slice_in_dim(value, 0, width, axis=dim)
        before = lax.ppermute(last, axis, up)
        after = lax.ppermute(first, axis, down)
        value = jnp.concatenate([before, value, after], axis=dim)
    return value


def apply_residual(padded, potential):
    center = padded[:, 1:-1].astype(jnp.float32)
    neighbours = padded[:, 2:].astype(jnp.float32) + padded[:, :-2].astype(jnp.float32)
    shaped = center.reshape(center.shape[0], center.shape[1], -1, NZ)
    across = (
        jnp.roll(shaped, 1, 2)
        + jnp.roll(shaped, -1, 2)
        + jnp.roll(shaped, 1, 3)
        + jnp.roll(shaped, -1, 3)
    )
    laplacian = neighbours + across.reshape(center.shape) - 6.0 * center
    resid = -0.5 * laplacian + potential[None] * center
    return (center, resid)


def shards(psi, ritz_matrix, potential):
    band_count = psi.shape[0]
    planes_dev = psi.shape[1]
    face_cells = psi.shape[2]
    piece = lax.all_gather(psi, "band", axis=0, tiled=True)
    flattened = piece.reshape(piece.shape[0], -1).astype(jnp.float32)
    folded = jnp.dot(ritz_matrix, flattened, precision=lax.Precision.HIGHEST)
    rotated = folded.reshape(band_count, planes_dev, face_cells).astype(jnp.bfloat16)
    padded = with_halo(rotated, (("grid", 1),), 1)
    center, resid = apply_residual(padded, potential)
    total_cells = planes_dev * face_cells * lax.axis_size("grid")
    cross_local = jnp.sum(center * resid, axis=(1, 2))
    self_local = jnp.sum(center * center, axis=(1, 2))
    resid_local = jnp.sum(resid * resid, axis=(1, 2))
    cross_sum, self_sum, resid_sum = lax.psum((cross_local, self_local, resid_local), "grid")
    m_cross = cross_sum / total_cells
    m_plain = self_sum / total_cells
    ratio = m_cross / (m_plain + epsilon_mean)
    direction = resid - ratio[:, None, None] * center
    m_dir = resid_sum / total_cells - 2.0 * ratio * m_cross + ratio * ratio * m_plain
    search = direction * lax.rsqrt(m_dir + epsilon_mean)[:, None, None]
    return (rotated, search.astype(jnp.bfloat16))


def solution(mesh):
    return jax.shard_map(
        shards,
        mesh=mesh,
        in_specs=(P("band", "grid", None), P("band", None), P("grid", None)),
        out_specs=(P("band", "grid", None), P("band", "grid", None)),
        check_vma=False,
    )
```

profile of v0, /device:TPU:0, one launch (start us, length us, event | category | flops | bytes accessed | tf_op | source)
XLA Modules:
  0.0 136.8 jit_solution(16779906986271277849)
XLA Ops:
  7.2 0.0 all-gather.2.cloned.1.call-start
  7.2 0.7 all-gather.2.cloned.1.call-update
  7.9 38.8 %all-gather.2.cloned.1.call-done = bf16[2048,2,512]{2,1,0:T(2,128)(2,1)} async-done(((bf16[512,2,512]{2,1,0:T(2,128)(2,1)}), bf16[2048,2,512]{2,1,0:T(2,128)(2,1)}) %all-gather.2.cloned.1.call-update) | async-done | bytes 4194320 | tf_op jit(solution)/shard_map/all_gather | solution.py:42
  46.7 11.2 %copy.11 = bf16[2048,2,512]{0,2,1:T(8,128)(2,1)} copy(bf16[2048,2,512]{2,1,0:T(2,128)(2,1)} %all-gather.2.cloned.1.call-done) | data formatting | bytes 8388608 | tf_op jit(solution)/shard_map/reshape | solution.py:43
  58.0 9.8 %fusion.13 = bf16[512,2,512]{0,2,1:T(8,128)(2,1)S(1)} fusion(bf16[2048,2,512]{0,2,1:T(8,128)(2,1)} %copy.11, f32[512,2048]{1,0:T(8,128)} %param.4), kind=kOutput, calls=%fused_computation.21 | convolution fusion | flops 12885426176 | bytes 9437184 | tf_op jit(solution)/shard_map/dot_general | solution.py:44
  67.8 2.5 %fusion.19 = (f32[512,2,8,63]{0,3,2,1:T(8,128)}, f32[512,2,8,63]{0,3,2,1:T(8,128)}) fusion(bf16[512,2,8,64]{0,3,2,1:T(8,128)(2,1)S(1)} %bitcast.26), kind=kLoop, calls=%fused_computation.27 | loop fusion | bytes 8257536 | tf_op jit(solution)/shard_map/jit(_roll_static)/slice | solution.py:31
  70.3 0.8 fusion.22
  71.2 1.0 fusion.18
  72.2 2.1 %copy.9 = bf16[512,2,512]{2,1,0:T(2,128)(2,1)} copy(bf16[512,2,512]{0,2,1:T(8,128)(2,1)S(1)} %fusion.13) | data formatting | bytes 2097152
  74.3 4.2 %collective-permute-start = (bf16[512,1,512]{0,2,1:T(8,128)(2,1)}, bf16[512,1,512]{0,2,1:T(8,128)(2,1)S(1)}, u32[]{:S(2)}, u32[]{:S(2)}) collective-permute-start(bf16[512,1,512]{0,2,1:T(8,128)(2,1)} %get-tuple-element.12), channel_id=1, source_target_pairs={{4,0},{8,4},{12,8},{16,12},{20,16},{24,20},{28,24},{0,28},{5,1},{9... | collective-permute-start | bytes 1572872 | tf_op jit(solution)/shard_map/ppermute | solution.py:18
  78.5 0.0 copy-start
  78.5 0.0 copy-start.1
  78.5 0.0 copy-start.4
  78.5 0.0 collective-permute-start.1
  78.5 0.5 fusion.21
  79.0 1.1 copy-done
  80.1 0.6 copy-done.1
  80.7 0.0 copy-done.4
  80.7 0.0 copy-start.5
  80.7 1.1 fusion.12
  81.8 18.0 %collective-permute-done = bf16[512,1,512]{0,2,1:T(8,128)(2,1)S(1)} collective-permute-done((bf16[512,1,512]{0,2,1:T(8,128)(2,1)}, bf16[512,1,512]{0,2,1:T(8,128)(2,1)S(1)}, u32[]{:S(2)}, u32[]{:S(2)}) %collective-permute-start) | collective-permute-done | bytes 524320 | tf_op jit(solution)/shard_map/ppermute | solution.py:18
  99.8 0.0 copy-start.2
  99.8 0.0 collective-permute-done.1
  99.8 0.0 copy-done.5
  99.8 0.0 copy-start.3
  99.8 1.3 fusion.6
  101.1 0.0 copy-done.2
  101.2 0.0 copy-done.3
  101.2 21.9 %all-reduce = (f32[512]{0:T(512)S(1)}, f32[512]{0:T(512)S(1)}, f32[512]{0:T(512)S(1)}) all-reduce(f32[512]{0:T(512)S(1)} %get-tuple-element.7, f32[512]{0:T(512)S(1)} %get-tuple-element.8, f32[512]{0:T(512)S(1)} %get-tuple-element.6), channel_id=1, replica_groups=mesh['grid'=8,'band'=4] {'grid'}, use_global_device_ids=true, to_apply=%region_5.6 | all-reduce | flops 1536 | bytes 12288 | tf_op jit(solution)/shard_map/psum | solution.py:52
  123.1 3.2 %fusion.10 = bf16[512,2,512]{0,2,1:T(8,128)(2,1)} fusion(bf16[512,2,512]{0,2,1:T(8,128)(2,1)S(1)} %fusion.13, f32[512]{0:T(512)S(1)} %get-tuple-element.23, f32[512]{0:T(512)S(1)} %get-tuple-element.22, f32[2,512]{1,0:T(2,128)S(1)} %copy-done.5, f32[512,2,8,64]{0,3,2,1:T(8,128)S(1)} %fusion.12, bf16[512,1,512]{0,2,1:T(8,128)(2,1)} %copy-done.3, ...), kind=kLoop, calls=%fused_computation.15 | loop fusion | flops 8388608 | bytes 5251072 | tf_op jit(solution)/shard_map/convert_element_type | solution.py:59
  126.3 3.7 %copy.10 = bf16[512,2,512]{2,1,0:T(2,128)(2,1)} copy(bf16[512,2,512]{0,2,1:T(8,128)(2,1)} %fusion.10) | data formatting | bytes 2097152
  (2 shorter events, 0.1 us)
Async XLA Ops:
  7.2 39.6 %all-gather.2.cloned.1.call-start = ((), (), s32[]{:S(2)}) async-start(), calls=%async_computation | async-start | bytes 5242880 | tf_op jit(solution)/shard_map/all_gather | solution.py:42
  74.3 25.5 %collective-permute-start = (bf16[512,1,512]{0,2,1:T(8,128)(2,1)}, bf16[512,1,512]{0,2,1:T(8,128)(2,1)S(1)}, u32[]{:S(2)}, u32[]{:S(2)}) collective-permute-start(bf16[512,1,512]{0,2,1:T(8,128)(2,1)} %get-tuple-element.12), channel_id=1, source_target_pairs={{4,0},{8,4},{12,8},{16,12},{20,16},{24,20},{28,24},{0,28},{5,1},{9... | collective-permute-start | bytes 1572872 | tf_op jit(solution)/shard_map/ppermute | solution.py:18
  78.5 1.6 %copy-start = (f32[512,2,8,63]{0,3,2,1:T(8,128)S(1)}, f32[512,2,8,63]{0,3,2,1:T(8,128)}, u32[]{:S(2)}) copy-start(f32[512,2,8,63]{0,3,2,1:T(8,128)} %get-tuple-element.14) | copy-start | bytes 6193156
  78.5 2.2 %copy-start.1 = (f32[512,2,8,63]{0,3,2,1:T(8,128)S(1)}, f32[512,2,8,63]{0,3,2,1:T(8,128)}, u32[]{:S(2)}) copy-start(f32[512,2,8,63]{0,3,2,1:T(8,128)} %get-tuple-element.15) | copy-start | bytes 6193156
  78.5 2.2 %copy-start.4 = (f32[512,2,1,64]{0,3,2,1:T(8,128)S(1)}, f32[512,2,1,64]{0,3,2,1:T(8,128)}, u32[]{:S(2)}) copy-start(f32[512,2,1,64]{0,3,2,1:T(8,128)} %get-tuple-element.21) | copy-start | bytes 786436
  78.5 21.3 %collective-permute-start.1 = (bf16[512,1,512]{0,2,1:T(8,128)(2,1)}, bf16[512,1,512]{0,2,1:T(8,128)(2,1)S(1)}, u32[]{:S(2)}, u32[]{:S(2)}) collective-permute-start(bf16[512,1,512]{0,2,1:T(8,128)(2,1)} %get-tuple-element.13), channel_id=1, source_target_pairs={{0,4},{4,8},{8,12},{12,16},{16,20},{20,24},{24,28},{28,0},{1,5},{5... | collective-permute-start | bytes 1572872 | tf_op jit(solution)/shard_map/ppermute | solution.py:17
  80.7 19.1 %copy-start.5 = (f32[2,512]{1,0:T(2,128)S(1)}, f32[2,512]{1,0:T(2,128)}, u32[]{:S(2)}) copy-start(f32[2,512]{1,0:T(2,128)} %param.5) | copy-start | bytes 12292
  99.8 1.4 copy-start.2
  99.8 1.4 copy-start.3
Sparse Core Ops, SparseCore 0:
  9.5 37.1 all-gather.1
where the time goes:
time: 137 us
  waiting for transfers between devices  57.5 us (42%)
  local copies, waits for them, and re-layouts  23.6 us (17%)
  blocking collectives  21.9 us (16%)
  between operations  14.1 us (10%)
  matrix products  9.83 us (7%)
  other arithmetic  5.62 us (4%)
  starting transfers between devices  4.28 us (3%)
    all_gather x1, waiting for transfers between devices, shards(): piece = lax.all_gather(psi, 'band', axis=0, tiled=True)  38.8 us
    psum x1, blocking collectives, shards(): lax.psum((cross_local, self_local, resid_local), 'grid')  21.9 us
    ppermute x1, waiting for transfers between devices, with_halo(): after = lax.ppermute(first, axis, down)  18 us
    reshape x1, local copies, waits for them, and re-layouts, shards(): flattened = piece.reshape(piece.shape[0], -1).astype(jnp.float32)  11.2 us
    dot_general x1, matrix products, shards(): folded = jnp.dot(ritz_matrix, flattened, precision=lax.Precision.HIGHEST)  9.83 us
    unnamed x14, local copies, waits for them, and re-layouts  7.49 us
    ppermute x1, starting transfers between devices, with_halo(): after = lax.ppermute(first, axis, down)  4.24 us
    convert_element_type x1, other arithmetic, shards(): return (rotated, search.astype(jnp.bfloat16))  3.19 us
  transfers between devices with their start and end apart: 3, of which 2 were waited for; matrix products, arithmetic and copies ran while one was open for 1% of the time, Pallas kernels for 0%

commit v1 on v0

--- a/solution.py
+++ b/solution.py
@@ -39,7 +39,13 @@
     band_count = psi.shape[0]
     planes_dev = psi.shape[1]
     face_cells = psi.shape[2]
-    piece = lax.all_gather(psi, "band", axis=0, tiled=True)
+    peers = lax.axis_size("band")
+    moving, pieces = (psi, [psi])
+    for _ in range(peers - 1):
+        moving = lax.ppermute(moving, "band", [(i_2, (i_2 + 1) % peers) for i_2 in range(peers)])
+        pieces.insert(0, moving)
+    flat = jnp.concatenate(pieces, axis=0)
+    piece = jnp.roll(flat, (lax.axis_index("band") + 1) * psi.shape[0], axis=0)
     flattened = piece.reshape(piece.shape[0], -1).astype(jnp.float32)
     folded = jnp.dot(ritz_matrix, flattened, precision=lax.Precision.HIGHEST)
     rotated = folded.reshape(band_count, planes_dev, face_cells).astype(jnp.bfloat16)

time: 137 us -> 122 us (0.89)
  between operations: 14.1 us -> 0.75 us
  waiting for transfers between devices: 57.5 us -> 62.3 us
  local copies, waits for them, and re-layouts: 23.6 us -> 20.6 us
  other arithmetic: 5.62 us -> 3.73 us
  matrix products: 9.83 us -> 8.04 us
  starting transfers between devices: 4.28 us -> 6.03 us
    ppermute x0 -> x3, waiting for transfers between devices: none -> 43 us  [shards(): lax.ppermute(moving, 'band', [(i_2, (i_2 + 1) % peers) for i_2 in range(p...]
    all_gather x1 -> x0, waiting for transfers between devices: 38.8 us -> none  [shards(): piece = lax.all_gather(psi, 'band', axis=0, tiled=True)]
    ppermute x1, waiting for transfers between devices: 0.01 us -> 17 us  [with_halo(): before = lax.ppermute(last, axis, up)]
    ppermute x1, waiting for transfers between devices: 18 us -> 2.21 us  [with_halo(): after = lax.ppermute(first, axis, down)]
    reshape x1 -> x0, local copies, waits for them, and re-layouts: 11.2 us -> none  [shards(): flattened = piece.reshape(piece.shape[0], -1).astype(jnp.float32)]
    unnamed x14 -> x20, local copies, waits for them, and re-layouts: 7.49 us -> 13.4 us
    dynamic_slice x0 -> x1, local copies, waits for them, and re-layouts: none -> 3.19 us  [shards(): piece = jnp.roll(flat, (lax.axis_index('band') + 1) * psi.shape[0], axis=0)]
    ppermute x1, starting transfers between devices: 0.01 us -> 2.32 us  [with_halo(): before = lax.ppermute(last, axis, up)]
  transfers between devices with their start and end apart: 3 -> 5, of which waited for: 2 -> 5; matrix products, arithmetic and copies ran while one was open for 1% -> 1% of each run, Pallas kernels for 0% -> 0%
where the time goes in v1:
time: 122 us
  waiting for transfers between devices  62.3 us (51%)
  blocking collectives  20.7 us (17%)
  local copies, waits for them, and re-layouts  20.6 us (17%)
  matrix products  8.04 us (7%)
  starting transfers between devices  6.03 us (5%)
  other arithmetic  3.73 us (3%)
    ppermute x3, waiting for transfers between devices, shards(): lax.ppermute(moving, 'band', [(i_2, (i_2 + 1) % peers) for i_2 in range(p...  43 us
    psum x1, blocking collectives, shards(): lax.psum((cross_local, self_local, resid_local), 'grid')  20.7 us
    ppermute x1, waiting for transfers between devices, with_halo(): before = lax.ppermute(last, axis, up)  17 us
    unnamed x20, local copies, waits for them, and re-layouts  13.4 us
    dot_general x1, matrix products, shards(): folded = jnp.dot(ritz_matrix, flattened, precision=lax.Precision.HIGHEST)  8.04 us
    dynamic_slice x1, local copies, waits for them, and re-layouts, shards(): piece = jnp.roll(flat, (lax.axis_index('band') + 1) * psi.shape[0], axis=0)  3.19 us
    ppermute x1, starting transfers between devices, with_halo(): after = lax.ppermute(first, axis, down)  3.12 us
  transfers between devices with their start and end apart: 5, of which 5 were waited for; matrix products, arithmetic and copies ran while one was open for 1% of the time, Pallas kernels for 0%

profile of v1, /device:TPU:0, one launch (start us, length us, event | category | flops | bytes accessed | tf_op | source)
XLA Modules:
  0.0 122.1 jit_solution(5828988405431060337)
XLA Ops:
  0.6 0.5 collective-permute-start
  1.2 14.6 %collective-permute-done = bf16[512,2,512]{2,1,0:T(2,128)(2,1)S(1)} collective-permute-done((bf16[512,2,512]{2,1,0:T(2,128)(2,1)}, bf16[512,2,512]{2,1,0:T(2,128)(2,1)S(1)}, u32[]{:S(2)}, u32[]{:S(2)}) %collective-permute-start) | collective-permute-done | bytes 1048608 | tf_op jit(solution)/shard_map/ppermute | solution.py:45
  15.8 0.0 collective-permute-start.1
  15.9 14.2 %collective-permute-done.1 = bf16[512,2,512]{2,1,0:T(2,128)(2,1)S(1)} collective-permute-done((bf16[512,2,512]{2,1,0:T(2,128)(2,1)S(1)}, bf16[512,2,512]{2,1,0:T(2,128)(2,1)S(1)}, u32[]{:S(2)}, u32[]{:S(2)}) %collective-permute-start.1) | collective-permute-done | bytes 1048608 | tf_op jit(solution)/shard_map/ppermute | solution.py:45
  30.0 0.0 collective-permute-start.2
  30.0 14.2 %collective-permute-done.2 = bf16[512,2,512]{2,1,0:T(2,128)(2,1)S(1)} collective-permute-done((bf16[512,2,512]{2,1,0:T(2,128)(2,1)S(1)}, bf16[512,2,512]{2,1,0:T(2,128)(2,1)S(1)}, u32[]{:S(2)}, u32[]{:S(2)}) %collective-permute-start.2) | collective-permute-done | bytes 1048608 | tf_op jit(solution)/shard_map/ppermute | solution.py:45
  44.3 0.7 constant_dynamic-update-slice_fusion.7
  45.0 0.0 copy-start.1
  45.0 0.8 constant_dynamic-update-slice_fusion.6
  45.8 0.8 constant_dynamic-update-slice_fusion.5
  46.6 0.0 copy-done.1
  46.6 0.8 constant_dynamic-update-slice_fusion.4
  47.4 0.8 constant_dynamic-update-slice_fusion.3
  48.2 0.8 constant_dynamic-update-slice_fusion.2
  49.0 0.8 constant_dynamic-update-slice_fusion.1
  49.7 0.8 constant_dynamic-update-slice_fusion
  50.5 3.2 %constant_dynamic-slice_fusion = bf16[2048,2,512]{2,1,0:T(2,128)(2,1)S(1)} fusion(bf16[4096,2,512]{2,1,0:T(2,128)(2,1)S(1)} %constant_dynamic-update-slice_fusion, s32[]{:T(128)S(6)} %select_n.14), kind=kLoop, calls=%fused_computation.30 | loop fusion | bytes 8388612 | tf_op jit(solution)/shard_map/jit(_roll_dynamic)/dynamic_slice | solution.py:48
  53.7 0.0 copy-start.4
  53.7 1.2 copy.14
  54.9 1.0 copy-done.4
  55.9 8.0 %multiply_reduce_fusion.1 = (f32[512]{0:T(512)S(1)}, bf16[1024,512]{1,0:T(8,128)(2,1)S(1)}) fusion(bf16[2048,1024]{1,0:T(8,128)(2,1)S(1)} %bitcast.25, f32[512,2048]{1,0:T(8,128)S(1)} %copy-done.4), kind=kOutput, calls=%fused_computation.16 | convolution fusion | flops 12886999040 | bytes 9439232 | tf_op jit(solution)/shard_map/dot_general | solution.py:50
  64.0 0.8 fusion.14
  64.7 1.9 %fusion.11 = (f32[512,2,8,63]{0,3,2,1:T(8,128)S(1)}, f32[512,2,8,63]{0,3,2,1:T(8,128)}) fusion(bf16[512,2,8,64]{0,3,2,1:T(8,128)(2,1)S(1)} %bitcast.18), kind=kLoop, calls=%fused_computation.32 | loop fusion | bytes 8257536 | tf_op jit(solution)/shard_map/jit(_roll_static)/slice | solution.py:31
  66.7 2.1 %copy.12 = bf16[512,2,512]{2,1,0:T(2,128)(2,1)} copy(bf16[512,2,512]{0,2,1:T(8,128)(2,1)S(1)} %bitcast.20) | data formatting | bytes 2097152
  68.8 0.1 fusion.10
  68.8 2.3 %collective-permute-start.4 = (bf16[512,1,512]{0,2,1:T(8,128)(2,1)S(1)}, bf16[512,1,512]{0,2,1:T(8,128)(2,1)S(1)}, u32[]{:S(2)}, u32[]{:S(2)}) collective-permute-start(bf16[512,1,512]{0,2,1:T(8,128)(2,1)S(1)} %get-tuple-element.13), channel_id=1, source_target_pairs={{0,4},{4,8},{8,12},{12,16},{16,20},{20,24},{24,28},{28,0},{1,5},{5... | collective-permute-start | bytes 1572872 | tf_op jit(solution)/shard_map/ppermute | solution.py:17
  71.2 0.0 copy-start
  71.2 0.0 copy-start.2
  71.2 3.1 %collective-permute-start.3 = (bf16[512,1,512]{0,2,1:T(8,128)(2,1)S(1)}, bf16[512,1,512]{0,2,1:T(8,128)(2,1)S(1)}, u32[]{:S(2)}, u32[]{:S(2)}) collective-permute-start(bf16[512,1,512]{0,2,1:T(8,128)(2,1)S(1)} %get-tuple-element.12), channel_id=1, source_target_pairs={{4,0},{8,4},{12,8},{16,12},{20,16},{24,20},{28,24},{0,28},{5,1},{9... | collective-permute-start | bytes 1572872 | tf_op jit(solution)/shard_map/ppermute | solution.py:18
  74.3 0.5 fusion.13
  74.8 0.0 copy-done
  74.8 0.0 copy-done.2
  74.8 0.0 copy-start.3
  74.8 1.1 fusion.8
  75.9 17.0 %collective-permute-done.4 = bf16[512,1,512]{0,2,1:T(8,128)(2,1)S(1)} collective-permute-done((bf16[512,1,512]{0,2,1:T(8,128)(2,1)S(1)}, bf16[512,1,512]{0,2,1:T(8,128)(2,1)S(1)}, u32[]{:S(2)}, u32[]{:S(2)}) %collective-permute-start.4) | collective-permute-done | bytes 524320 | tf_op jit(solution)/shard_map/ppermute | solution.py:17
  92.9 2.2 %collective-permute-done.3 = bf16[512,1,512]{0,2,1:T(8,128)(2,1)S(1)} collective-permute-done((bf16[512,1,512]{0,2,1:T(8,128)(2,1)S(1)}, bf16[512,1,512]{0,2,1:T(8,128)(2,1)S(1)}, u32[]{:S(2)}, u32[]{:S(2)}) %collective-permute-start.3) | collective-permute-done | bytes 524320 | tf_op jit(solution)/shard_map/ppermute | solution.py:18
  95.1 0.0 copy-done.3
  95.1 1.3 %fusion.3 = (f32[512]{0:T(512)S(1)}, f32[512]{0:T(512)S(1)}, f32[512,2,512]{0,2,1:T(8,128)S(1)}) fusion(bf16[1024,512]{1,0:T(8,128)(2,1)S(1)} %get-tuple-element.25, f32[2,512]{1,0:T(2,128)S(1)} %copy-done.3, bf16[512,2,512]{0,2,1:T(8,128)(2,1)S(1)} %bitcast.23, f32[512,2,8,64]{0,3,2,1:T(8,128)S(1)} %fusion.8, ...), kind=kLoop, calls=%fused_computation.7 | loop fusion | flops 8911872 | bytes 7348224 | tf_op jit(solution)/shard_map/reduce_sum | solution.py:55
  96.4 20.7 %all-reduce = (f32[512]{0:T(512)S(1)}, f32[512]{0:T(512)S(1)}, f32[512]{0:T(512)S(1)}) all-reduce(f32[512]{0:T(512)S(1)} %get-tuple-element.7, f32[512]{0:T(512)S(1)} %get-tuple-element.24, f32[512]{0:T(512)S(1)} %get-tuple-element.6), channel_id=1, replica_groups=mesh['grid'=8,'band'=4] {'grid'}, use_global_device_ids=true, to_apply=%region_5.6 | all-reduce | flops 1536 | bytes 12288 | tf_op jit(solution)/shard_map/psum | solution.py:58
  117.1 1.4 %fusion.6 = bf16[512,2,512]{0,2,1:T(8,128)(2,1)} fusion(f32[512,2,512]{0,2,1:T(8,128)S(1)} %get-tuple-element.11, f32[512]{0:T(512)S(1)} %get-tuple-element.23, f32[512]{0:T(512)S(1)} %get-tuple-element.22, bf16[1024,512]{1,0:T(8,128)(2,1)S(1)} %get-tuple-element.25), kind=kLoop, calls=%fused_computation.10 | loop fusion | flops 2621440 | bytes 4198400 | tf_op jit(solution)/shard_map/convert_element_type | solution.py:65
  118.4 3.7 %copy.13 = bf16[512,2,512]{2,1,0:T(2,128)(2,1)} copy(bf16[512,2,512]{0,2,1:T(8,128)(2,1)} %fusion.6) | data formatting | bytes 2097152
  (2 shorter events, 0.1 us)
Async XLA Ops:
  0.6 15.2 %collective-permute-start = (bf16[512,2,512]{2,1,0:T(2,128)(2,1)}, bf16[512,2,512]{2,1,0:T(2,128)(2,1)S(1)}, u32[]{:S(2)}, u32[]{:S(2)}) collective-permute-start(bf16[512,2,512]{2,1,0:T(2,128)(2,1)} %param.3), channel_id=1, source_target_pairs={{0,1},{1,2},{2,3},{3,0},{4,5},{5,6},{6,7},{7,4},{8,9},{9,10},{10,1... | collective-permute-start | bytes 3145736 | tf_op jit(solution)/shard_map/ppermute | solution.py:45
  15.8 14.2 %collective-permute-start.1 = (bf16[512,2,512]{2,1,0:T(2,128)(2,1)S(1)}, bf16[512,2,512]{2,1,0:T(2,128)(2,1)S(1)}, u32[]{:S(2)}, u32[]{:S(2)}) collective-permute-start(bf16[512,2,512]{2,1,0:T(2,128)(2,1)S(1)} %collective-permute-done), channel_id=1, source_target_pairs={{0,1},{1,2},{2,3},{3,0},{4,5},{5,6},{6,7},{7,4},{8,9},{9,10},{10,1... | collective-permute-start | bytes 3145736 | tf_op jit(solution)/shard_map/ppermute | solution.py:45
  30.0 14.2 %collective-permute-start.2 = (bf16[512,2,512]{2,1,0:T(2,128)(2,1)S(1)}, bf16[512,2,512]{2,1,0:T(2,128)(2,1)S(1)}, u32[]{:S(2)}, u32[]{:S(2)}) collective-permute-start(bf16[512,2,512]{2,1,0:T(2,128)(2,1)S(1)} %collective-permute-done.1), channel_id=1, source_target_pairs={{0,1},{1,2},{2,3},{3,0},{4,5},{5,6},{6,7},{7,4},{8,9},{9,10},{10,1... | collective-permute-start | bytes 3145736 | tf_op jit(solution)/shard_map/ppermute | solution.py:45
  45.0 1.6 %copy-start.1 = (bf16[512,2,512]{2,1,0:T(2,128)(2,1)S(1)}, bf16[512,2,512]{2,1,0:T(2,128)(2,1)}, u32[]{:S(2)}) copy-start(bf16[512,2,512]{2,1,0:T(2,128)(2,1)} %param.3) | copy-start | bytes 3145732
  53.7 2.2 %copy-start.4 = (f32[512,2048]{1,0:T(8,128)S(1)}, f32[512,2048]{1,0:T(8,128)}, u32[]{:S(2)}) copy-start(f32[512,2048]{1,0:T(8,128)} %param.4) | copy-start | bytes 12582916
  68.8 24.1 %collective-permute-start.4 = (bf16[512,1,512]{0,2,1:T(8,128)(2,1)S(1)}, bf16[512,1,512]{0,2,1:T(8,128)(2,1)S(1)}, u32[]{:S(2)}, u32[]{:S(2)}) collective-permute-start(bf16[512,1,512]{0,2,1:T(8,128)(2,1)S(1)} %get-tuple-element.13), channel_id=1, source_target_pairs={{0,4},{4,8},{8,12},{12,16},{16,20},{20,24},{24,28},{28,0},{1,5},{5... | collective-permute-start | bytes 1572872 | tf_op jit(solution)/shard_map/ppermute | solution.py:17
  71.2 3.6 %copy-start = (f32[512,2,8,63]{0,3,2,1:T(8,128)S(1)}, f32[512,2,8,63]{0,3,2,1:T(8,128)}, u32[]{:S(2)}) copy-start(f32[512,2,8,63]{0,3,2,1:T(8,128)} %get-tuple-element.15) | copy-start | bytes 6193156
  71.2 3.6 %copy-start.2 = (f32[512,2,1,64]{0,3,2,1:T(8,128)S(1)}, f32[512,2,1,64]{0,3,2,1:T(8,128)}, u32[]{:S(2)}) copy-start(f32[512,2,1,64]{0,3,2,1:T(8,128)} %get-tuple-element.21) | copy-start | bytes 786436
  71.2 23.9 %collective-permute-start.3 = (bf16[512,1,512]{0,2,1:T(8,128)(2,1)S(1)}, bf16[512,1,512]{0,2,1:T(8,128)(2,1)S(1)}, u32[]{:S(2)}, u32[]{:S(2)}) collective-permute-start(bf16[512,1,512]{0,2,1:T(8,128)(2,1)S(1)} %get-tuple-element.12), channel_id=1, source_target_pairs={{4,0},{8,4},{12,8},{16,12},{20,16},{24,20},{28,24},{0,28},{5,1},{9... | collective-permute-start | bytes 1572872 | tf_op jit(solution)/shard_map/ppermute | solution.py:18
  74.8 20.3 %copy-start.3 = (f32[2,512]{1,0:T(2,128)S(1)}, f32[2,512]{1,0:T(2,128)}, u32[]{:S(2)}) copy-start(f32[2,512]{1,0:T(2,128)} %param.5) | copy-start | bytes 12292
